TPU v7x, 256 devices: a whole 4x4x8 slice. The times are simulated.
256 devices in a mesh: row: 8 (over z), col: 8 (over y, core), depth: 4 (over x).
Axes of the slice: x: 4, y: 4, z: 8, core: 2. Of those that a mesh axis runs over, the one named last changes fastest.
Arguments:
- a21_leaf: float32 [4, 4096, 2048], P('depth', 'row', 'col'), may hold values from -1.2 to 1.2
- a12_leaf: float32 [4, 2048, 4096], P('depth', 'row', 'col'), may hold values from -1.2 to 1.2
- uinv_leaf: float32 [4, 2048, 2048], P('depth', None, 'col'), may hold values from -0.2 to 1.5, as said below
- linv_leaf: float32 [4, 2048, 2048], P('depth', 'row'), may hold values from -0.2 to 1.5, as said below
- live: int32 [4], P('depth'), may hold values from 16 to 32
- row_map: int32 [4, 32], P('depth', 'row'), may hold values from 0 to 63, as said below
- col_map: int32 [4, 32], P('depth', 'col'), may hold values from 0 to 63, as said below
- a22_anc: float32 [8192, 8192], P(('row', 'depth'), 'col'), may hold values from -6 to 6
- a21_anc: float32 [8192, 2048], P(('row', 'depth'), 'col'), may hold values from -1.2 to 1.2
- a12_anc: float32 [2048, 8192], P(('row', 'depth'), 'col'), may hold values from -1.2 to 1.2
- uinv_anc: float32 [2048, 2048], P(None, 'col'), may hold values from -0.2 to 1.5, as said below
- linv_anc: float32 [2048, 2048], P(('row', 'depth')), may hold values from -0.2 to 1.5, as said below
Outputs:
- leaf_lower: float32 [4, 4096, 2048], P('depth', 'row', 'col')
- leaf_upper: float32 [4, 2048, 4096], P('depth', 'row', 'col')
- anc_lower: float32 [8192, 2048], P(('row', 'depth'), 'col')
- anc_upper: float32 [2048, 8192], P(('row', 'depth'), 'col')
- anc_schur: float32 [8192, 8192], P(('row', 'depth'), 'col')
Inputs may be any that keep to these rules, and one draw needn't show every extreme that they name: `uinv_leaf`: upper triangular: zero below the diagonal, diagonal between 0.5 and 1.5. `linv_leaf`: lower triangular: zero above the diagonal, diagonal between 0.5 and 1.5. `uinv_anc`: upper triangular: zero below the diagonal, diagonal between 0.5 and 1.5. `linv_anc`: lower triangular: zero above the diagonal, diagonal between 0.5 and 1.5. `row_map`: within one replica the entries are distinct. Leaf block row i lies in the k-th of 8 equal ranges of leaf block rows, and its target lies in the k-th of 8 equal ranges of the 64 ancestor block rows. `col_map`: within one replica the entries are distinct. Leaf block column j lies in the k-th of 8 equal ranges of leaf block columns, and its target lies in the k-th of 8 equal ranges of the 64 ancestor block columns.
All inputs are finite; a program needn't handle non-finite values.
Results may differ from a plain program's by a relative error of at most 0.0001.
Values sent between devices are 32-bit elements; how exact they have to be, the bound alone decides.
No kernel may reach another device: no remote copies, remote signals or barrier semaphores. Data moves between devices by JAX's collectives and lax.ppermute only.
A program may use at most 128 MiB of HBM per device.

v0:
```python
import math
import jax
import jax.numpy as jnp
from jax import lax
from jax.sharding import PartitionSpec as P

NB = 128


def in_one_piece(arrays, axis, split_dim, concat_dim, along):
    widths = [math.prod(a.shape[along:]) for a in arrays]
    both = jnp.concatenate(
        [a.reshape(*a.shape[:along], w) for a, w in zip(arrays, widths)], axis=along
    )
    out = lax.all_to_all(both, axis, split_axis=split_dim, concat_axis=concat_dim, tiled=True)
    tiles = jnp.split(out, [sum(widths[:k]) for k in range(1, len(widths))], axis=along)
    return tuple((b.reshape(*out.shape[:along], *a.shape[along:]) for a, b in zip(arrays, tiles)))


def sent_to_all(shard, axis):
    copies = jnp.broadcast_to(shard, (lax.axis_size(axis), *shard.shape))
    return lax.all_to_all(copies, axis, split_axis=0, concat_axis=0, tiled=True)


def in_order(tiles, dim):
    lengths = list(tiles.shape[1:])
    lengths[dim] *= tiles.shape[0]
    return jnp.moveaxis(tiles, 0, dim).reshape(lengths)


def collect(shard, axis, dim):
    tiles = sent_to_all(shard, axis)
    return in_order(tiles, dim)


def gather_axes(shard, axes, dim):
    out = shard
    for number in range(len(axes) - 1, -1, -1):
        out = lax.all_gather(out, axes[number], axis=dim, tiled=True)
    return out


def product(left, right):
    return jnp.dot(left, right, precision=lax.Precision.HIGHEST, preferred_element_type=jnp.float32)


def combine_depth(schur, row_map, col_map, a22_anc):
    block_size = NB
    rows_here = schur.shape[0]
    cols_here = schur.shape[1]
    leaf_rows = rows_here // block_size
    leaf_cols = cols_here // block_size
    anc_rows = a22_anc.shape[0]
    replicas = lax.axis_size("depth")
    anc_row_blocks = anc_rows * replicas // block_size
    anc_col_blocks = a22_anc.shape[1] // block_size
    row_local = row_map[0] - lax.axis_index("row") * anc_row_blocks
    col_local = col_map[0] - lax.axis_index("col") * anc_col_blocks
    owner_blocks = anc_rows // block_size
    slots = min(leaf_rows, owner_blocks)
    owner = row_local // owner_blocks
    earlier = lax.iota(jnp.int32, leaf_rows)[:, None] > lax.iota(jnp.int32, leaf_rows)[None, :]
    same = owner[:, None] == owner[None, :]
    rank = jnp.sum((earlier & same).astype(jnp.int32), axis=1)
    select = (
        (owner[:, None, None] == lax.iota(jnp.int32, replicas)[None, :, None])
        & (rank[:, None, None] == lax.iota(jnp.int32, slots)[None, None, :])
    ).astype(jnp.float32)
    leaf_blocks = schur.reshape(leaf_rows, block_size, cols_here)
    packed = jnp.einsum("iqs,ixc->qsxc", select, leaf_blocks, precision=lax.Precision.HIGHEST)
    packed = packed.reshape(replicas, slots * block_size, cols_here)
    target = (row_local - owner * owner_blocks + 1).astype(jnp.float32)
    tags = jnp.einsum("iqs,i->qs", select, target, precision=lax.Precision.HIGHEST) - 1.0
    col_tags = jnp.broadcast_to(col_local.astype(jnp.float32)[None, :], (replicas, leaf_cols))
    got_rows, got_tags, got_cols = in_one_piece((packed, tags, col_tags), "depth", 0, 0, 1)
    slot_pick = (
        got_tags[:, :, None] == lax.iota(jnp.int32, owner_blocks).astype(jnp.float32)[None, None, :]
    ).astype(jnp.float32)
    column_pick = (
        got_cols[:, :, None]
        == lax.iota(jnp.int32, anc_col_blocks).astype(jnp.float32)[None, None, :]
    ).astype(jnp.float32)
    pieces = got_rows.reshape(replicas, slots, block_size, leaf_cols, block_size)
    sectioned = jnp.einsum("psa,psxjy->paxjy", slot_pick, pieces, precision=lax.Precision.HIGHEST)
    placed = jnp.einsum("paxjy,pjb->axby", sectioned, column_pick, precision=lax.Precision.HIGHEST)
    return placed.reshape(anc_rows, anc_col_blocks * block_size)


def anc_panels(a21_anc, a12_anc, uinv_anc, linv_anc):
    factor = uinv_anc
    anc_lower = product(collect(a21_anc, "col", 1), factor)
    lower_whole = collect(anc_lower, "col", 1)
    factor = linv_anc
    anc_upper = product(factor, lax.all_gather(a12_anc, ("row", "depth"), axis=0, tiled=True))
    return (anc_lower, lower_whole, anc_upper)


def shards(
    a21_leaf,
    a12_leaf,
    uinv_leaf,
    linv_leaf,
    live,
    row_map,
    col_map,
    a22_anc,
    a21_anc,
    a12_anc,
    uinv_anc,
    linv_anc,
):
    block_size = NB
    panel_left = a21_leaf[0]
    panel_top = a12_leaf[0]
    upper_inverse = uinv_leaf[0]
    lower_inverse = linv_leaf[0]
    rows_here = panel_left.shape[0]
    cols_here = panel_top.shape[1]
    live_rows = live[0] * block_size
    row_pos = lax.axis_index("row") * rows_here + lax.iota(jnp.int32, rows_here)
    col_pos = lax.axis_index("col") * cols_here + lax.iota(jnp.int32, cols_here)
    row_keep = (row_pos < live_rows).astype(jnp.float32)
    col_keep = (col_pos < live_rows).astype(jnp.float32)
    factor = upper_inverse
    lower_part = product(lax.all_gather(panel_left, "col", axis=1, tiled=True), factor)
    leaf_lower = lower_part * row_keep[:, None]
    factor = lower_inverse
    upper_part = product(factor, lax.all_gather(panel_top, "row", axis=0, tiled=True))
    leaf_upper = upper_part * col_keep[None, :]
    upper_whole = lax.all_gather(leaf_upper, "row", axis=0, tiled=True)
    factor = upper_whole
    schur = jnp.zeros((rows_here, cols_here), jnp.float32) - product(
        lax.all_gather(leaf_lower, "col", axis=1, tiled=True), factor
    )
    own_update = combine_depth(schur, row_map, col_map, a22_anc)
    anc_lower, lower_whole, anc_upper = anc_panels(a21_anc, a12_anc, uinv_anc, linv_anc)
    factor = lower_whole
    anc_schur = a22_anc + own_update - product(factor, gather_axes(anc_upper, ("row", "depth"), 0))
    return (leaf_lower[None], leaf_upper[None], anc_lower, anc_upper, anc_schur)


def solution(mesh):
    in_specs = (
        P("depth", "row", "col"),
        P("depth", "row", "col"),
        P("depth", None, "col"),
        P("depth", "row", None),
        P("depth"),
        P("depth", "row"),
        P("depth", "col"),
        P(("row", "depth"), "col"),
        P(("row", "depth"), "col"),
        P(("row", "depth"), "col"),
        P(None, "col"),
        P(("row", "depth"), None),
    )
    out_specs = (
        P("depth", "row", "col"),
        P("depth", "row", "col"),
        P(("row", "depth"), "col"),
        P(("row", "depth"), "col"),
        P(("row", "depth"), "col"),
    )
    return jax.shard_map(shards, mesh=mesh, in_specs=in_specs, out_specs=out_specs, check_vma=False)
```

profile of v0, /device:TPU:1, one launch (start us, length us, event | category | flops | bytes accessed | tf_op | source)
XLA Modules:
  0.0 436.7 jit_solution(4254180319421357973)
XLA Ops:
  7.2 0.0 all-gather.20.cloned.1.call-start
  7.2 0.7 all-gather.20.cloned.1.call-update
  7.9 0.0 all-gather.22.cloned.1.call-start
  8.0 0.7 all-gather.22.cloned.1.call-update
  8.7 0.0 all-gather.10.cloned.1.call-start
  8.7 0.7 all-gather.10.cloned.1.call-update
  9.4 0.0 all-gather.12.cloned.1.call-start
  10.1 38.6 %all-gather.20.cloned.1.call-done = f32[1,512,2048]{2,1,0:T(8,128)} async-done(((f32[1,512,256]{2,1,0:T(8,128)}), f32[1,512,2048]{2,1,0:T(8,128)}) %all-gather.20.cloned.1.call-update) | async-done | bytes 4194320 | tf_op jit(solution)/shard_map/all_gather | solution.py:125
  48.7 6.4 %fusion.10 = f32[512,256]{1,0:T(8,128)} fusion(f32[1,2048,256]{2,1,0:T(8,128)S(1)} %copy-done, f32[1,512,2048]{2,1,0:T(8,128)} %all-gather.20.cloned.1.call-done, f32[512]{0:T(512)S(1)} %fusion.32), kind=kOutput, calls=%fused_computation.13 | convolution fusion | flops 3221356544 | bytes 6817792 | tf_op jit(solution)/shard_map/dot_general | solution.py:44
  55.1 0.0 all-gather.12.cloned.1.call-update
  55.1 0.0 all-gather.14.cloned.1.call-start
  55.2 49.4 %all-gather.22.cloned.1.call-done = f32[1,2048,512]{2,1,0:T(8,128)} async-done(((f32[1,256,512]{2,1,0:T(8,128)}), f32[1,2048,512]{2,1,0:T(8,128)}) %all-gather.22.cloned.1.call-update) | async-done | bytes 4194320 | tf_op jit(solution)/shard_map/all_gather | solution.py:128
  104.6 7.3 %fusion.15 = f32[256,512]{1,0:T(8,128)} fusion(f32[1,2048,512]{2,1,0:T(8,128)} %all-gather.22.cloned.1.call-done, f32[1,256,2048]{2,1,0:T(8,128)} %param.15, f32[512]{0:T(512)S(1)} %fusion.33), kind=kOutput, calls=%fused_computation.14 | convolution fusion | flops 3221356544 | bytes 6817792 | tf_op jit(solution)/shard_map/dot_general | solution.py:44
  112.0 0.1 copy.29
  112.1 1.5 broadcast_in_dim.16
  113.6 5.3 %all-to-all-start = ((f32[8,256,256]{1,2,0:T(8,128)}), f32[8,256,256]{1,2,0:T(8,128)S(1)}, u32[]{:S(2)}, u32[]{:S(2)}) async-start(f32[8,256,256]{1,2,0:T(8,128)} %broadcast_in_dim.16), calls=%async_computation | async-start | bytes 4194304 | tf_op jit(solution)/shard_map/all_to_all | solution.py:22
  118.9 0.1 convert_reduce_fusion
  119.0 84.1 %all-gather.10.cloned.1.call-done = f32[2048,1024]{1,0:T(8,128)} async-done(((f32[64,1024]{1,0:T(8,128)}), f32[2048,1024]{1,0:T(8,128)}) %all-gather.10.cloned.1.call-update) | async-done | bytes 8388624 | tf_op jit(solution)/shard_map/all_gather | solution.py:94
  203.1 8.2 %fusion.51 = f32[64,1024]{1,0:T(8,128)} fusion(f32[64,2048]{1,0:T(8,128)S(1)} %copy-done.3, f32[2048,1024]{1,0:T(8,128)} %all-gather.10.cloned.1.call-done), kind=kOutput, calls=%fused_computation.69 | convolution fusion | flops 1610612736 | bytes 9175040 | tf_op jit(solution)/shard_map/dot_general | solution.py:44
  211.4 0.2 all-gather.18.cloned.1.call-start
  211.6 0.1 fusion.27
  211.7 0.1 copy.37
  211.8 0.1 bitcast_add_fusion.1
  211.9 26.4 %all-gather.12.cloned.1.call-done = f32[512,2048]{1,0:T(8,128)} async-done(((f32[512,256]{1,0:T(8,128)}), f32[512,2048]{1,0:T(8,128)}) %all-gather.12.cloned.1.call-update) | async-done | bytes 4194320 | tf_op jit(solution)/shard_map/all_gather | solution.py:133
  238.3 56.4 %all-gather.14.cloned.1.call-done = f32[2048,512]{1,0:T(8,128)} async-done(((f32[256,512]{1,0:T(8,128)}), f32[2048,512]{1,0:T(8,128)}) %all-gather.14.cloned.1.call-update) | async-done | bytes 4194320 | tf_op jit(solution)/shard_map/all_gather | solution.py:130
  294.7 9.4 %convolution_subtract_fusion = f32[512,512]{1,0:T(8,128)S(1)} fusion(f32[512,2048]{1,0:T(8,128)} %all-gather.12.cloned.1.call-done, f32[2048,512]{1,0:T(8,128)} %all-gather.14.cloned.1.call-done), kind=kOutput, calls=%fused_computation.11 | convolution fusion | flops 6442713088 | bytes 9437184 | tf_op jit(solution)/shard_map/dot_general | solution.py:44
  304.0 3.6 fusion.20
  307.6 12.7 %all-gather.16.cloned.1.call-done = f32[256,1024]{1,0:T(8,128)} async-done(((f32[64,1024]{1,0:T(8,128)}), f32[256,1024]{1,0:T(8,128)}) %all-gather.16.cloned.1.call-update) | async-done | bytes 1048592 | tf_op jit(solution)/shard_map/all_gather | solution.py:39
  320.3 3.1 constant_dynamic-update-slice_fusion
  323.4 1.3 dynamic-update-slice.1
  324.7 1.4 dynamic-update-slice.2
  326.0 4.8 %copy.31 = f32[4,1,131078]{2,1,0:T(1,128)} copy(f32[4,1,131078]{2,0,1:T(4,128)} %bitcast.99) | data formatting | bytes 4194496 | tf_op jit(solution)/shard_map/all_to_all | solution.py:15
  330.9 4.5 %all-to-all-start.1 = ((f32[4,1,131078]{2,1,0:T(1,128)}), f32[4,1,131078]{2,1,0:T(1,128)}, u32[]{:S(2)}, u32[]{:S(2)}) async-start(f32[4,1,131078]{2,1,0:T(1,128)} %copy.31), calls=%async_computation.1 | async-start | bytes 4198400 | tf_op jit(solution)/shard_map/all_to_all | solution.py:15
  335.4 5.3 %fusion.50 = f32[256,256]{1,0:T(8,128)S(1)} fusion(f32[256,2048]{0,1:T(8,128)S(1)} %bitcast.100, f32[2048,256]{1,0:T(8,128)} %param.22), kind=kOutput, calls=%fused_computation.68 | convolution fusion | flops 1610612736 | bytes 4456448 | tf_op jit(solution)/shard_map/dot_general | solution.py:44
  340.7 0.1 copy.35
  340.8 18.3 %all-to-all-done.1 = f32[4,1,131078]{2,1,0:T(1,128)} async-done(((f32[4,1,131078]{2,1,0:T(1,128)}), f32[4,1,131078]{2,1,0:T(1,128)}, u32[]{:S(2)}, u32[]{:S(2)}) %all-to-all-start.1) | async-done | bytes 2097280 | tf_op jit(solution)/shard_map/all_to_all | solution.py:15
  359.1 1.5 broadcast_in_dim.20
  360.6 7.9 %all-to-all-start.2 = ((f32[8,256,256]{1,2,0:T(8,128)}), f32[8,256,256]{1,2,0:T(8,128)}, u32[]{:S(2)}, u32[]{:S(2)}) async-start(f32[8,256,256]{1,2,0:T(8,128)} %broadcast_in_dim.20), calls=%async_computation.2 | async-start | bytes 4194304 | tf_op jit(solution)/shard_map/all_to_all | solution.py:22
  368.5 2.6 copy.53
  371.2 1.5 split.14
  372.7 0.1 split.12
  372.8 3.4 reshape_reshape.7
  376.2 0.1 copy.32
  376.2 4.8 %fusion.8 = f32[4,2,128,4,128]{4,1,3,2,0:T(2,128)S(1)} fusion(f32[4,2,128,4,128]{4,3,2,1,0:T(4,128)S(1)} %reshape_reshape.7, f32[4,2]{1,0:T(4,128)S(1)} %split.13, f32[2]{0:T(128)S(1)} %iota_convert_fusion), kind=kOutput, calls=%fused_computation.9 | convolution fusion | flops 12582928 | bytes 4194344 | tf_op jit(solution)/shard_map/psa,psxjy->paxjy/dot_general | solution.py:84
  381.0 3.2 fusion.6
  384.3 10.6 %all-to-all-done.2 = f32[8,256,256]{1,2,0:T(8,128)} async-done(((f32[8,256,256]{1,2,0:T(8,128)}), f32[8,256,256]{1,2,0:T(8,128)}, u32[]{:S(2)}, u32[]{:S(2)}) %all-to-all-start.2) | async-done | bytes 2097184 | tf_op jit(solution)/shard_map/all_to_all | solution.py:22
  394.8 23.6 %all-gather.18.cloned.1.call-done = f32[2048,1024]{1,0:T(8,128)} async-done(((f32[256,1024]{1,0:T(8,128)}), f32[2048,1024]{1,0:T(8,128)}) %all-gather.18.cloned.1.call-update) | async-done | bytes 8388624 | tf_op jit(solution)/shard_map/all_gather | solution.py:39
  418.5 11.4 %convolution_subtract_fusion.1 = f32[256,1024]{1,0:T(8,128)} fusion(f32[256,2048]{0,1:T(8,128)} %bitcast.28, f32[2048,1024]{1,0:T(8,128)} %all-gather.18.cloned.1.call-done, f32[256,1024]{1,0:T(8,128)} %param.19, f32[32,8,8,128]{3,2,1,0:T(8,128)S(1)} %bitcast.103), kind=kOutput, calls=%fused_computation.12 | convolution fusion | flops 6442975232 | bytes 13631488 | tf_op jit(solution)/shard_map/dot_general | solution.py:44
  (30 shorter events, 0.2 us)
Async XLA Ops:
  7.2 41.5 %copy-start = (f32[1,2048,256]{2,1,0:T(8,128)S(1)}, f32[1,2048,256]{2,1,0:T(8,128)}, u32[]{:S(2)}) copy-start(f32[1,2048,256]{2,1,0:T(8,128)} %param.14) | copy-start | bytes 6291460
  7.2 41.5 %all-gather.20.cloned.1.call-start = ((), (), s32[]{:S(2)}) async-start(), calls=%async_computation.8 | async-start | bytes 4718592 | tf_op jit(solution)/shard_map/all_gather | solution.py:125
  7.9 96.7 %all-gather.22.cloned.1.call-start = ((), (), s32[]{:S(2)}) async-start(), calls=%async_computation.9 | async-start | bytes 4718592 | tf_op jit(solution)/shard_map/all_gather | solution.py:128
  8.7 194.5 %all-gather.10.cloned.1.call-start = ((), (), s32[]{:S(2)}) async-start(), calls=%async_computation.3 | async-start | bytes 8650752 | tf_op jit(solution)/shard_map/all_gather | solution.py:94
  9.4 228.9 %all-gather.12.cloned.1.call-start = ((), (), s32[]{:S(2)}) async-start(), calls=%async_computation.4 | async-start | bytes 4718592 | tf_op jit(solution)/shard_map/all_gather | solution.py:133
  55.1 239.5 %all-gather.14.cloned.1.call-start = ((), (), s32[]{:S(2)}) async-start(), calls=%async_computation.5 | async-start | bytes 4718592 | tf_op jit(solution)/shard_map/all_gather | solution.py:130
  55.2 56.8 %copy-start.4 = (f32[256,256]{1,0:T(8,128)S(1)}, f32[256,256]{1,0:T(8,128)}, u32[]{:S(2)}) copy-start(f32[256,256]{1,0:T(8,128)} %param.20) | copy-start | bytes 786436
  113.6 5.3 %copy-start.5 = (s32[1,4]{1,0:T(1,128)S(1)}, s32[1,4]{1,0:T(1,128)}, u32[]{:S(2)}) copy-start(s32[1,4]{1,0:T(1,128)} %param.17) | copy-start | bytes 52
  113.6 89.5 %copy-start.3 = (f32[64,2048]{1,0:T(8,128)S(1)}, f32[64,2048]{1,0:T(8,128)}, u32[]{:S(2)}) copy-start(f32[64,2048]{1,0:T(8,128)} %param.23) | copy-start | bytes 1572868
  113.6 217.2 %all-to-all-start = ((f32[8,256,256]{1,2,0:T(8,128)}), f32[8,256,256]{1,2,0:T(8,128)S(1)}, u32[]{:S(2)}, u32[]{:S(2)}) async-start(f32[8,256,256]{1,2,0:T(8,128)} %broadcast_in_dim.16), calls=%async_computation | async-start | bytes 4194304 | tf_op jit(solution)/shard_map/all_to_all | solution.py:22
  118.9 201.4 %all-gather.16.cloned.1.call-start = ((), (), s32[]{:S(2)}) async-start(), calls=%async_computation.6 | async-start | bytes 1310720 | tf_op jit(solution)/shard_map/all_gather | solution.py:39
  119.0 92.8 %copy-start.6 = (s32[1,4]{1,0:T(1,128)S(1)}, s32[1,4]{1,0:T(1,128)}, u32[]{:S(2)}) copy-start(s32[1,4]{1,0:T(1,128)} %param.18) | copy-start | bytes 52
  211.4 207.1 %all-gather.18.cloned.1.call-start = ((), (), s32[]{:S(2)}) async-start(), calls=%async_computation.7 | async-start | bytes 9437184 | tf_op jit(solution)/shard_map/all_gather | solution.py:39
  330.9 28.3 %all-to-all-start.1 = ((f32[4,1,131078]{2,1,0:T(1,128)}), f32[4,1,131078]{2,1,0:T(1,128)}, u32[]{:S(2)}, u32[]{:S(2)}) async-start(f32[4,1,131078]{2,1,0:T(1,128)} %copy.31), calls=%async_computation.1 | async-start | bytes 4198400 | tf_op jit(solution)/shard_map/all_to_all | solution.py:15
  340.7 20.0 %copy-start.2 = (f32[256,256]{1,0:T(8,128)}, f32[256,256]{1,0:T(8,128)S(1)}, u32[]{:S(2)}) copy-start(f32[256,256]{1,0:T(8,128)S(1)} %fusion.50) | copy-start | bytes 786436
  360.6 34.2 %all-to-all-start.2 = ((f32[8,256,256]{1,2,0:T(8,128)}), f32[8,256,256]{1,2,0:T(8,128)}, u32[]{:S(2)}, u32[]{:S(2)}) async-start(f32[8,256,256]{1,2,0:T(8,128)} %broadcast_in_dim.20), calls=%async_computation.2 | async-start | bytes 4194304 | tf_op jit(solution)/shard_map/all_to_all | solution.py:22
  418.5 11.4 %copy-start.1 = (f32[1,2048,256]{2,1,0:T(8,128)S(1)}, f32[1,2048,256]{2,1,0:T(8,128)}, u32[]{:S(2)}) copy-start(f32[1,2048,256]{2,1,0:T(8,128)} %param.14) | copy-start | bytes 6291460
Sparse Core Ops, SparseCore 0:
  9.8 38.8 all-gather.19
  50.5 54.1 all-gather.21
  107.2 95.8 all-gather.9
  205.4 32.8 all-gather.11
  240.5 54.1 all-gather.13
  296.9 23.3 all-gather.15
  322.0 96.3 all-gather.17
where the time goes:
time: 437 us
  waiting for transfers between devices  322 us (74%)
  matrix products  59.7 us (14%)
  local copies, waits for them, and re-layouts  21.7 us (5%)
  starting transfers between devices  18.1 us (4%)
  between operations  14.9 us (3%)
    all_gather x1, waiting for transfers between devices, anc_panels(): lax.all_gather(a12_anc, ('row', 'depth'), axis=0, tiled=True)  84.1 us
    all_gather x1, waiting for transfers between devices, shards(): upper_whole = lax.all_gather(leaf_upper, 'row', axis=0, tiled=True)  56.4 us
    all_gather x1, waiting for transfers between devices, shards(): lax.all_gather(panel_top, 'row', axis=0, tiled=True)  49.4 us
    dot_general x6, matrix products, product(): jnp.dot(left, right, precision=lax.Precision.HIGHEST, preferred_element_t...  48 us
    all_gather x1, waiting for transfers between devices, shards(): lax.all_gather(panel_left, 'col', axis=1, tiled=True)  38.6 us
    all_gather x2, waiting for transfers between devices, gather_axes(): out = lax.all_gather(out, axes[number], axis=dim, tiled=True)  36.3 us
    all_gather x1, waiting for transfers between devices, shards(): lax.all_gather(leaf_lower, 'col', axis=1, tiled=True)  26.4 us
    all_to_all x1, waiting for transfers between devices, in_one_piece(): lax.all_to_all(both, axis, split_axis=split_dim, concat_axis=concat_dim,...  18.3 us
  transfers between devices with their start and end apart: 10, of which 9 were waited for; matrix products, arithmetic and copies ran while one was open for 16% of the time, Pallas kernels for 0%

commit v1 on v0

--- a/solution.py
+++ b/solution.py
@@ -5,6 +5,11 @@
 from jax.sharding import PartitionSpec as P
 
 NB = 128
+
+
+def gather_by_exchange(x, axis, dim):
+    copies = jnp.concatenate([x] * lax.axis_size(axis), axis=dim)
+    return lax.all_to_all(copies, axis, dim, dim, tiled=True)
 
 
 def in_one_piece(arrays, axis, split_dim, concat_dim, along):
@@ -91,7 +96,7 @@
     anc_lower = product(collect(a21_anc, "col", 1), factor)
     lower_whole = collect(anc_lower, "col", 1)
     factor = linv_anc
-    anc_upper = product(factor, lax.all_gather(a12_anc, ("row", "depth"), axis=0, tiled=True))
+    anc_upper = product(factor, gather_by_exchange(a12_anc, ("row", "depth"), 0))
     return (anc_lower, lower_whole, anc_upper)
 
 

time: 437 us -> 481 us (1.10); the launches traced: 437 us -> 472 us
  local copies, waits for them, and re-layouts: 21.7 us -> 37 us
  starting transfers between devices: 18.1 us -> 31.9 us
    all_gather x1 -> x0, waiting for transfers between devices: 84.1 us -> none  [anc_panels(): lax.all_gather(a12_anc, ('row', 'depth'), axis=0, tiled=True)]
    all_to_all x0 -> x1, waiting for transfers between devices: none -> 83 us  [gather_by_exchange(): return lax.all_to_all(copies, axis, dim, dim, tiled=True)]
    all_gather x1, waiting for transfers between devices: 56.4 us -> 2.01 us  [shards(): upper_whole = lax.all_gather(leaf_upper, 'row', axis=0, tiled=True)]
    all_gather x1, waiting for transfers between devices: 49.4 us -> 95.9 us  [shards(): lax.all_gather(panel_top, 'row', axis=0, tiled=True)]
    unnamed x18 -> x53, local copies, waits for them, and re-layouts: 7.18 us -> 24.2 us
    all_to_all x0 -> x1, starting transfers between devices: none -> 12 us  [gather_by_exchange(): return lax.all_to_all(copies, axis, dim, dim, tiled=True)]
    all_gather x1, waiting for transfers between devices: 26.4 us -> 35.1 us  [shards(): lax.all_gather(leaf_lower, 'col', axis=1, tiled=True)]
  transfers between devices with their start and end apart: 10 -> 10, of which waited for: 9 -> 9; matrix products, arithmetic and copies ran while one was open for 16% -> 18% of each run, Pallas kernels for 0% -> 0%
where the time goes in v1:
time: 481 us; the launch traced here: 472 us
  waiting for transfers between devices  325 us (68%)
  matrix products  62 us (13%)
  local copies, waits for them, and re-layouts  37 us (8%)
  starting transfers between devices  31.9 us (7%)
  between operations  15.5 us (3%)
    all_gather x1, waiting for transfers between devices, shards(): lax.all_gather(panel_top, 'row', axis=0, tiled=True)  95.9 us
    all_to_all x1, waiting for transfers between devices, gather_by_exchange(): return lax.all_to_all(copies, axis, dim, dim, tiled=True)  83 us
    dot_general x6, matrix products, product(): jnp.dot(left, right, precision=lax.Precision.HIGHEST, preferred_element_t...  48.4 us
    all_gather x2, waiting for transfers between devices, gather_axes(): out = lax.all_gather(out, axes[number], axis=dim, tiled=True)  40.4 us
    all_gather x1, waiting for transfers between devices, shards(): lax.all_gather(panel_left, 'col', axis=1, tiled=True)  38.7 us
    all_gather x1, waiting for transfers between devices, shards(): lax.all_gather(leaf_lower, 'col', axis=1, tiled=True)  35.1 us
    unnamed x53, local copies, waits for them, and re-layouts  24.2 us
    all_to_all x1, waiting for transfers between devices, in_one_piece(): lax.all_to_all(both, axis, split_axis=split_dim, concat_axis=concat_dim,...  18.3 us
  transfers between devices with their start and end apart: 10, of which 9 were waited for; matrix products, arithmetic and copies ran while one was open for 18% of the time, Pallas kernels for 0%

profile of v1, /device:TPU:1, one launch (start us, length us, event | category | flops | bytes accessed | tf_op | source)
XLA Modules:
  0.0 471.6 jit_solution(13604882796122553320)
XLA Ops:
  7.2 0.7 all-gather.19.cloned.1.call-update
  8.0 0.7 all-gather.17.cloned.1.call-update
  8.7 1.0 constant_dynamic-update-slice_fusion.31
  9.7 1.0 constant_dynamic-update-slice_fusion.30
  10.6 1.0 constant_dynamic-update-slice_fusion.29
  11.6 1.0 constant_dynamic-update-slice_fusion.28
  12.6 1.0 constant_dynamic-update-slice_fusion.27
  13.5 1.0 constant_dynamic-update-slice_fusion.26
  14.5 1.0 constant_dynamic-update-slice_fusion.25
  15.5 1.0 constant_dynamic-update-slice_fusion.24
  16.5 1.0 constant_dynamic-update-slice_fusion.23
  17.4 1.0 constant_dynamic-update-slice_fusion.22
  18.4 1.0 constant_dynamic-update-slice_fusion.21
  19.4 1.0 constant_dynamic-update-slice_fusion.20
  20.4 1.0 constant_dynamic-update-slice_fusion.19
  21.3 1.0 constant_dynamic-update-slice_fusion.18
  22.8 3.2 copy-done.3
  26.1 12.0 %all-to-all-start.1 = ((f32[32,64,1024]{2,1,0:T(8,128)}), f32[32,64,1024]{2,1,0:T(8,128)}, u32[]{:S(2)}, u32[]{:S(2)}) async-start(f32[32,64,1024]{2,1,0:T(8,128)} %bitcast.100), calls=%async_computation.1 | async-start | bytes 16777216 | tf_op jit(solution)/shard_map/all_to_all | solution.py:12
  38.8 95.9 %all-gather.19.cloned.1.call-done = f32[1,2048,512]{2,1,0:T(8,128)} async-done(((f32[1,256,512]{2,1,0:T(8,128)}), f32[1,2048,512]{2,1,0:T(8,128)}) %all-gather.19.cloned.1.call-update) | async-done | bytes 4194320 | tf_op jit(solution)/shard_map/all_gather | solution.py:133
  134.7 6.7 %fusion.15 = f32[256,512]{1,0:T(8,128)} fusion(f32[1,2048,512]{2,1,0:T(8,128)} %all-gather.19.cloned.1.call-done, f32[1,256,2048]{2,1,0:T(8,128)S(1)} %copy-done, f32[512]{0:T(512)S(1)} %fusion.33), kind=kOutput, calls=%fused_computation.14 | convolution fusion | flops 3221356544 | bytes 6817792 | tf_op jit(solution)/shard_map/dot_general | solution.py:49
  141.5 38.7 %all-gather.17.cloned.1.call-done = f32[1,512,2048]{2,1,0:T(8,128)} async-done(((f32[1,512,256]{2,1,0:T(8,128)}), f32[1,512,2048]{2,1,0:T(8,128)}) %all-gather.17.cloned.1.call-update) | async-done | bytes 4194320 | tf_op jit(solution)/shard_map/all_gather | solution.py:130
  180.2 7.1 %fusion.10 = f32[512,256]{1,0:T(8,128)} fusion(f32[1,2048,256]{2,1,0:T(8,128)} %param.14, f32[1,512,2048]{2,1,0:T(8,128)} %all-gather.17.cloned.1.call-done, f32[512]{0:T(512)S(1)} %fusion.32), kind=kOutput, calls=%fused_computation.13 | convolution fusion | flops 3221356544 | bytes 6817792 | tf_op jit(solution)/shard_map/dot_general | solution.py:49
  187.6 83.0 %all-to-all-done.1 = f32[32,64,1024]{2,1,0:T(8,128)} async-done(((f32[32,64,1024]{2,1,0:T(8,128)}), f32[32,64,1024]{2,1,0:T(8,128)}, u32[]{:S(2)}, u32[]{:S(2)}) %all-to-all-start.1) | async-done | bytes 8388640 | tf_op jit(solution)/shard_map/all_to_all | solution.py:12
  270.6 1.5 broadcast_in_dim.16
  272.1 6.6 %all-to-all-start = ((f32[8,256,256]{1,2,0:T(8,128)}), f32[8,256,256]{1,2,0:T(8,128)S(1)}, u32[]{:S(2)}, u32[]{:S(2)}) async-start(f32[8,256,256]{1,2,0:T(8,128)} %broadcast_in_dim.16), calls=%async_computation | async-start | bytes 4194304 | tf_op jit(solution)/shard_map/all_to_all | solution.py:27
  278.7 8.5 %convolution_bitcast_fusion = f32[64,1024]{1,0:T(8,128)} fusion(f32[2048,1024]{1,0:T(8,128)} %bitcast.10, f32[64,2048]{1,0:T(8,128)S(1)} %copy-done.5), kind=kOutput, calls=%fused_computation.15 | convolution fusion | flops 1610612736 | bytes 9175040 | tf_op jit(solution)/shard_map/dot_general | solution.py:49
  287.2 0.5 all-gather.15.cloned.1.call-start
  288.0 2.0 all-gather.11.cloned.1.call-done
  290.0 35.1 %all-gather.9.cloned.1.call-done = f32[512,2048]{1,0:T(8,128)} async-done(((f32[512,256]{1,0:T(8,128)}), f32[512,2048]{1,0:T(8,128)}) %all-gather.9.cloned.1.call-update) | async-done | bytes 4194320 | tf_op jit(solution)/shard_map/all_gather | solution.py:138
  325.2 9.3 %convolution_subtract_fusion = f32[512,512]{1,0:T(8,128)S(1)} fusion(f32[512,2048]{1,0:T(8,128)} %all-gather.9.cloned.1.call-done, f32[2048,512]{1,0:T(8,128)} %all-gather.11.cloned.1.call-done), kind=kOutput, calls=%fused_computation.11 | convolution fusion | flops 6442713088 | bytes 9437184 | tf_op jit(solution)/shard_map/dot_general | solution.py:49
  334.5 3.6 fusion.20
  338.1 16.9 %all-gather.13.cloned.1.call-done = f32[256,1024]{1,0:T(8,128)} async-done(((f32[64,1024]{1,0:T(8,128)}), f32[256,1024]{1,0:T(8,128)}) %all-gather.13.cloned.1.call-update) | async-done | bytes 1048592 | tf_op jit(solution)/shard_map/all_gather | solution.py:44
  355.0 3.1 constant_dynamic-update-slice_fusion.32
  358.1 1.2 dynamic-update-slice.1
  359.3 1.2 dynamic-update-slice.2
  360.5 4.8 %copy.31 = f32[4,1,131078]{2,1,0:T(1,128)} copy(f32[4,1,131078]{2,0,1:T(4,128)} %bitcast.104) | data formatting | bytes 4194496 | tf_op jit(solution)/shard_map/all_to_all | solution.py:20
  365.3 4.5 all-to-all-start.2
  369.9 5.3 %fusion.50 = f32[256,256]{1,0:T(8,128)S(1)} fusion(f32[256,2048]{0,1:T(8,128)S(1)} %bitcast.105, f32[2048,256]{1,0:T(8,128)} %param.22), kind=kOutput, calls=%fused_computation.101 | convolution fusion | flops 1610612736 | bytes 4456448 | tf_op jit(solution)/shard_map/dot_general | solution.py:49
  375.3 18.3 %all-to-all-done.2 = f32[4,1,131078]{2,1,0:T(1,128)} async-done(((f32[4,1,131078]{2,1,0:T(1,128)}), f32[4,1,131078]{2,1,0:T(1,128)}, u32[]{:S(2)}, u32[]{:S(2)}) %all-to-all-start.2) | async-done | bytes 2097280 | tf_op jit(solution)/shard_map/all_to_all | solution.py:20
  393.6 1.5 broadcast_in_dim.20
  395.1 8.1 %all-to-all-start.3 = ((f32[8,256,256]{1,2,0:T(8,128)}), f32[8,256,256]{1,2,0:T(8,128)}, u32[]{:S(2)}, u32[]{:S(2)}) async-start(f32[8,256,256]{1,2,0:T(8,128)} %broadcast_in_dim.20), calls=%async_computation.3 | async-start | bytes 4194304 | tf_op jit(solution)/shard_map/all_to_all | solution.py:27
  403.3 2.6 copy.53
  406.1 3.2 reshape_reshape.7
  409.4 6.7 %fusion.8 = f32[4,2,128,4,128]{4,1,3,2,0:T(2,128)S(1)} fusion(f32[4,2,128,4,128]{4,3,2,1,0:T(4,128)} %reshape_reshape.7, f32[4,2]{1,0:T(4,128)S(1)} %split.13, f32[2]{0:T(128)S(1)} %iota_convert_fusion), kind=kOutput, calls=%fused_computation.9 | convolution fusion | flops 12582928 | bytes 4194344 | tf_op jit(solution)/shard_map/psa,psxjy->paxjy/dot_general | solution.py:89
  416.1 3.2 fusion.6
  419.4 10.1 %all-to-all-done.3 = f32[8,256,256]{1,2,0:T(8,128)} async-done(((f32[8,256,256]{1,2,0:T(8,128)}), f32[8,256,256]{1,2,0:T(8,128)}, u32[]{:S(2)}, u32[]{:S(2)}) %all-to-all-start.3) | async-done | bytes 2097184 | tf_op jit(solution)/shard_map/all_to_all | solution.py:27
  429.5 23.6 %all-gather.15.cloned.1.call-done = f32[2048,1024]{1,0:T(8,128)} async-done(((f32[256,1024]{1,0:T(8,128)}), f32[2048,1024]{1,0:T(8,128)}) %all-gather.15.cloned.1.call-update) | async-done | bytes 8388624 | tf_op jit(solution)/shard_map/all_gather | solution.py:44
  453.0 11.5 %convolution_subtract_fusion.1 = f32[256,1024]{1,0:T(8,128)} fusion(f32[256,2048]{0,1:T(8,128)} %bitcast.31, f32[2048,1024]{1,0:T(8,128)} %all-gather.15.cloned.1.call-done, f32[256,1024]{1,0:T(8,128)} %param.19, f32[32,8,8,128]{3,2,1,0:T(8,128)S(1)} %bitcast.108), kind=kOutput, calls=%fused_computation.12 | convolution fusion | flops 6442975232 | bytes 13631488 | tf_op jit(solution)/shard_map/dot_general | solution.py:49
  (65 shorter events, 1.6 us)
Async XLA Ops:
  7.2 127.6 %copy-start = (f32[1,256,2048]{2,1,0:T(8,128)S(1)}, f32[1,256,2048]{2,1,0:T(8,128)}, u32[]{:S(2)}) copy-start(f32[1,256,2048]{2,1,0:T(8,128)} %param.15) | copy-start | bytes 6291460
  7.2 15.1 %copy-start.2 = (f32[64,1024]{1,0:T(8,128)S(1)}, f32[64,1024]{1,0:T(8,128)}, u32[]{:S(2)}) copy-start(f32[64,1024]{1,0:T(8,128)} %param.21) | copy-start | bytes 786436
  7.2 127.5 %all-gather.19.cloned.1.call-start = ((), (), s32[]{:S(2)}) async-start(), calls=%async_computation.9 | async-start | bytes 4718592 | tf_op jit(solution)/shard_map/all_gather | solution.py:133
  7.9 172.3 %all-gather.17.cloned.1.call-start = ((), (), s32[]{:S(2)}) async-start(), calls=%async_computation.8 | async-start | bytes 4718592 | tf_op jit(solution)/shard_map/all_gather | solution.py:130
  22.8 3.2 copy-start.3
  26.1 244.5 %all-to-all-start.1 = ((f32[32,64,1024]{2,1,0:T(8,128)}), f32[32,64,1024]{2,1,0:T(8,128)}, u32[]{:S(2)}, u32[]{:S(2)}) async-start(f32[32,64,1024]{2,1,0:T(8,128)} %bitcast.100), calls=%async_computation.1 | async-start | bytes 16777216 | tf_op jit(solution)/shard_map/all_to_all | solution.py:12
  38.0 149.3 %copy-start.6 = (f32[256,256]{1,0:T(8,128)S(1)}, f32[256,256]{1,0:T(8,128)}, u32[]{:S(2)}) copy-start(f32[256,256]{1,0:T(8,128)} %param.20) | copy-start | bytes 786436
  38.1 149.4 %copy-start.7 = (s32[1,4]{1,0:T(1,128)S(1)}, s32[1,4]{1,0:T(1,128)}, u32[]{:S(2)}) copy-start(s32[1,4]{1,0:T(1,128)} %param.17) | copy-start | bytes 52
  38.1 252.0 %all-gather.11.cloned.1.call-start = ((), (), s32[]{:S(2)}) async-start(), calls=%async_computation.5 | async-start | bytes 4718592 | tf_op jit(solution)/shard_map/all_gather | solution.py:135
  141.4 137.3 %copy-start.5 = (f32[64,2048]{1,0:T(8,128)S(1)}, f32[64,2048]{1,0:T(8,128)}, u32[]{:S(2)}) copy-start(f32[64,2048]{1,0:T(8,128)} %param.23) | copy-start | bytes 1572868
  141.4 183.8 %all-gather.9.cloned.1.call-start = ((), (), s32[]{:S(2)}) async-start(), calls=%async_computation.4 | async-start | bytes 4718592 | tf_op jit(solution)/shard_map/all_gather | solution.py:138
  187.3 100.7 %copy-start.8 = (s32[1,4]{1,0:T(1,128)S(1)}, s32[1,4]{1,0:T(1,128)}, u32[]{:S(2)}) copy-start(s32[1,4]{1,0:T(1,128)} %param.18) | copy-start | bytes 52
  272.1 93.3 %all-to-all-start = ((f32[8,256,256]{1,2,0:T(8,128)}), f32[8,256,256]{1,2,0:T(8,128)S(1)}, u32[]{:S(2)}, u32[]{:S(2)}) async-start(f32[8,256,256]{1,2,0:T(8,128)} %broadcast_in_dim.16), calls=%async_computation | async-start | bytes 4194304 | tf_op jit(solution)/shard_map/all_to_all | solution.py:27
  278.7 76.3 %all-gather.13.cloned.1.call-start = ((), (), s32[]{:S(2)}) async-start(), calls=%async_computation.6 | async-start | bytes 1310720 | tf_op jit(solution)/shard_map/all_gather | solution.py:44
  287.2 165.8 %all-gather.15.cloned.1.call-start = ((), (), s32[]{:S(2)}) async-start(), calls=%async_computation.7 | async-start | bytes 9437184 | tf_op jit(solution)/shard_map/all_gather | solution.py:44
  365.3 28.3 %all-to-all-start.2 = ((f32[4,1,131078]{2,1,0:T(1,128)}), f32[4,1,131078]{2,1,0:T(1,128)}, u32[]{:S(2)}, u32[]{:S(2)}) async-start(f32[4,1,131078]{2,1,0:T(1,128)} %copy.31), calls=%async_computation.2 | async-start | bytes 4198400 | tf_op jit(solution)/shard_map/all_to_all | solution.py:20
  375.1 34.2 %copy-start.4 = (f32[256,256]{1,0:T(8,128)}, f32[256,256]{1,0:T(8,128)S(1)}, u32[]{:S(2)}) copy-start(f32[256,256]{1,0:T(8,128)S(1)} %fusion.50) | copy-start | bytes 786436
  395.1 34.4 %all-to-all-start.3 = ((f32[8,256,256]{1,2,0:T(8,128)}), f32[8,256,256]{1,2,0:T(8,128)}, u32[]{:S(2)}, u32[]{:S(2)}) async-start(f32[8,256,256]{1,2,0:T(8,128)} %broadcast_in_dim.20), calls=%async_computation.3 | async-start | bytes 4194304 | tf_op jit(solution)/shard_map/all_to_all | solution.py:27
  409.4 55.2 %copy-start.1 = (f32[1,256,2048]{2,1,0:T(8,128)S(1)}, f32[1,256,2048]{2,1,0:T(8,128)}, u32[]{:S(2)}) copy-start(f32[1,256,2048]{2,1,0:T(8,128)} %param.15) | copy-start | bytes 6291460
Sparse Core Ops, SparseCore 0:
  9.8 124.9 all-gather.18
  136.6 43.5 all-gather.16
  182.6 107.4 all-gather.10
  292.3 32.8 all-gather.8
  327.4 27.5 all-gather.12
  356.6 96.3 all-gather.14
